TPU v7x, 256 devices: a whole 4x4x8 slice. The times are simulated.
256 devices in a mesh: blk: 64 (over z, y_hi, x), deg: 4 (over y_lo, core).
Axes of the slice: x: 4, y: 4 (y_hi: 2, y_lo: 2; y = y_hi * 2 + y_lo), z: 8, core: 2. Of those that a mesh axis runs over, the one named last changes fastest.
Arguments:
- source: bfloat16 [672, 16384], P('deg', 'blk'), may hold values from -6 to 6
- operators: bfloat16 [12, 672, 672], replicated, may hold values from -0.125 to 0.125
- mie_factor: float32 [672, 16384], P('deg', 'blk'), may hold values from 0.3 to 1.5
- pair_source: int32 [6, 4, 16384], P(None, None, 'blk'), may hold values from 0 to 255
- pair_class: int32 [6, 4, 16384], P(None, None, 'blk'), may hold values from 0 to 11
- pair_scale: bfloat16 [6, 4, 16384], P(None, None, 'blk'), may hold values from 0.25 to 1
Outputs:
- result: float32 [672, 16384], P('deg', 'blk')
Inputs may be any that keep to these rules, and one draw needn't show every extreme that they name: `pair_source`: index of a source sphere within the visited block.
All inputs are finite; a program needn't handle non-finite values.
Results may differ from a plain program's by a relative error of at most 0.0075.
Values may be sent and summed in bfloat16 or wider, within the bound.
No kernel may reach another device: no remote copies, remote signals or barrier semaphores. Data moves between devices by JAX's collectives and lax.ppermute only.
A program may use at most 64 MiB of HBM per device.

v0:
```python
import functools

import jax
import jax.numpy as jnp
from jax import lax
from jax.experimental import pallas as pl
from jax.experimental.pallas import tpu as pltpu
from jax.sharding import PartitionSpec as P


LANES = 128
STRIP = 64
ORDER = (0, 1, 2, 3, 4, 5)
EARLY = 4
SPHERE_BITS = 8
SCALE_BITS = 10
SCALE_UNIT = 512
DEPTH = 256
LEAD = 8
VMEM = pl.BlockSpec(memory_space=pltpu.VMEM)


def column_windows(full, rows):
    windows = []
    for d in range(full // rows):
        start = d * rows // LANES * LANES
        if (d + 1) * rows - start > DEPTH:
            start += LANES
        windows.append((start, min(DEPTH, full - start), d * rows - start))
        assert windows[-1][2] >= -LEAD and windows[-1][2] % 8 == 0
    return windows


def prepare(codes, operators, table, weights, extra, stage, arrived):
    classes, full, _ = operators.shape
    visits, slots, spheres = codes.shape
    rows = full // lax.axis_size("deg")
    deg = lax.axis_index("deg")
    windows = column_windows(full, rows)

    def window(d, c):
        start, length, _ = windows[d]
        if length == DEPTH:
            return pltpu.make_async_copy(operators.at[c, :, start : start + length], weights.at[c], arrived.at[c])
        return pltpu.make_async_copy(operators.at[c], stage.at[c], arrived.at[c])

    def each_group(body):
        for d in range(full // rows):
            pl.when(deg == d)(functools.partial(body, d))

    def fetch(d):
        for c in range(classes):
            window(d, c).start()

    each_group(fetch)

    def spread(x):
        return [jnp.broadcast_to(x[k : k + 1, :], (LEAD, spheres)) for k in range(slots)]

    def strip(tile):
        return jnp.concatenate([tile] * (STRIP // LEAD), axis=0)

    zero = jnp.zeros((), jnp.bfloat16)
    sphere = lax.broadcasted_iota(jnp.int32, (STRIP, spheres), 0).astype(jnp.float32).astype(jnp.bfloat16)

    def tables(s, _):
        kind = jnp.right_shift(codes[s], SPHERE_BITS + SCALE_BITS)
        picked = jnp.bitwise_and(jnp.right_shift(codes[s], SCALE_BITS), 2**SPHERE_BITS - 1)
        scale = jnp.bitwise_and(codes[s], 2**SCALE_BITS - 1).astype(jnp.float32) * (1.0 / SCALE_UNIT)
        picked = [strip(x) for x in spread(picked.astype(jnp.float32).astype(jnp.bfloat16))]
        scale = [strip(x) for x in spread(scale.astype(jnp.bfloat16))]
        kind = spread(kind.astype(jnp.float32).astype(jnp.bfloat16))
        one = jnp.ones((), jnp.bfloat16)
        mine = [[strip(jnp.where(x == jnp.asarray(c, x.dtype), one, zero)) for x in kind] for c in range(classes)]
        for start in range(0, spheres, STRIP):
            here = sphere + jnp.asarray(start, jnp.bfloat16)
            hits = [jnp.where(here == picked[k], scale[k], zero) for k in range(slots)]
            for c in range(classes):
                terms = [hits[k] * mine[c][k] for k in range(slots)]
                while len(terms) > 1:
                    terms = [sum(terms[i + 1 : i + 2], terms[i]) for i in range(0, len(terms), 2)]
                table[c, s, start : start + STRIP] = terms[0]
        return 0

    lax.fori_loop(0, visits, tables, 0)

    def finish(d):
        start, length, first_row = windows[d]
        whole = length // LANES * LANES
        row = lax.broadcasted_iota(jnp.int32, (LANES, extra.shape[1]), 0) - (LANES + first_row)
        column = lax.broadcasted_iota(jnp.int32, (LANES, extra.shape[1]), 1)
        before = None
        for c in range(classes):
            window(d, c).wait()
            if length < DEPTH:
                weights[c, :, :whole] = stage[c, :, start : start + whole]
                weights[c, :, whole:] = jnp.zeros((full, DEPTH - whole), jnp.bfloat16)
                weights[c, :, whole:length] = stage[c, :, start + whole : start + length]
            if first_row < 0:
                pick = jnp.where((row >= 0) & (row + LEAD * c == column), 1.0, 0.0).astype(jnp.bfloat16)
                term = jnp.dot(stage[c, :, start - LANES : start], pick, preferred_element_type=jnp.float32)
                before = term if before is None else before + term
        extra[...] = jnp.zeros_like(extra) if before is None else before.astype(jnp.bfloat16)

    each_group(finish)


def add_visits(start, visiting, table, visits, c):
    for s, block in zip(visits, visiting):
        term = jnp.dot(block[...], table[c, s], preferred_element_type=jnp.float32)
        start = term if start is None else start + term
    return start


def gather_early(visits, *refs):
    *visiting, table, early = refs
    for c in range(table.shape[0]):
        early[c] = add_visits(None, visiting, table, visits, c)


def field_of(weights, extra, combined, slot):
    rows = extra.shape[0] // lax.axis_size("deg")
    chunk = pl.ds(pl.multiple_of(jnp.bitwise_xor(lax.axis_index("deg"), slot) * rows, 8), rows)
    lead = jnp.concatenate([combined[c, :LEAD] for c in range(weights.shape[0])], axis=0)
    field = jnp.dot(extra[chunk], lead, preferred_element_type=jnp.float32)
    for c in range(weights.shape[0]):
        field += jnp.dot(weights[c, chunk], combined[c, LEAD:], preferred_element_type=jnp.float32)
    return field


def interact_far(visits, slots, *refs):
    early, *visiting, table, weights, extra, combined = refs[: len(refs) - len(slots)]
    rows = early.shape[1]
    place = jnp.int32(LEAD)
    for d, (_, _, first_row) in enumerate(column_windows(weights.shape[1], rows)):
        place += jnp.where(lax.axis_index("deg") == d, first_row, 0)
    combined[...] = jnp.zeros_like(combined)
    for c in range(table.shape[0]):
        mixed = add_visits(early[c], visiting, table, visits, c)
        combined[c, pl.ds(pl.multiple_of(place, 8), rows)] = mixed.astype(jnp.bfloat16)
    for slot, out in zip(slots, refs[len(refs) - len(slots) :]):
        out[...] = field_of(weights, extra, combined, slot).astype(out.dtype)


def interact_near(slots, weights, extra, combined, *outs):
    for slot, out in zip(slots, outs):
        out[...] = field_of(weights, extra, combined, slot).astype(out.dtype)


def local(source, operators, mie_factor, pair_source, pair_class, pair_scale):
    rows, spheres = source.shape
    classes, full, _ = operators.shape
    visits = pair_source.shape[0]
    groups = full // rows
    blocks = lax.axis_size("blk")
    visiting = [source]
    for s in range(1, visits):
        visiting.append(lax.ppermute(source, "blk", [(b, (b + s) % blocks) for b in range(blocks)]))

    units = (pair_scale.astype(jnp.float32) * SCALE_UNIT).astype(jnp.int32)
    codes = (pair_class * 2**SPHERE_BITS + pair_source) * 2**SCALE_BITS + units
    table, weights, extra = pl.pallas_call(
        prepare,
        out_shape=(
            jax.ShapeDtypeStruct((classes, visits, spheres, spheres), jnp.bfloat16),
            jax.ShapeDtypeStruct((classes, full, DEPTH), jnp.bfloat16),
            jax.ShapeDtypeStruct((full, LEAD * classes), jnp.bfloat16),
        ),
        in_specs=[VMEM, pl.BlockSpec(memory_space=pl.ANY)],
        out_specs=(VMEM,) * 3,
        scratch_shapes=[
            pltpu.VMEM((classes, full, full), jnp.bfloat16),
            pltpu.SemaphoreType.DMA((classes,)),
        ],
        compiler_params=pltpu.CompilerParams(vmem_limit_bytes=40 * 2**20),
        cost_estimate=pl.CostEstimate(
            flops=2 * classes * full * full * rows, bytes_accessed=2 * operators.size, transcendentals=0
        ),
        name="prepare",
    )(codes, operators)

    def call(kernel, out_shape, flops, *operands):
        return pl.pallas_call(
            kernel,
            out_shape=out_shape,
            in_specs=[VMEM] * len(operands),
            out_specs=jax.tree.map(lambda _: VMEM, out_shape),
            compiler_params=pltpu.CompilerParams(vmem_limit_bytes=16 * 2**20),
            cost_estimate=pl.CostEstimate(flops=flops, bytes_accessed=2 * source.size, transcendentals=0),
        )(*operands)

    def shape(dtype, *lead):
        return jax.ShapeDtypeStruct((*lead, rows, spheres), dtype)

    gather = 2 * rows * spheres * spheres * classes
    product = 2 * rows * rows * spheres * classes
    first, late = ORDER[:EARLY], ORDER[EARLY:]
    early = call(
        functools.partial(gather_early, first),
        shape(jnp.float32, classes),
        len(first) * gather,
        *(visiting[s] for s in first),
        table,
    )

    def exchange(x, distance):
        return lax.ppermute(x, "deg", [(i, i ^ distance) for i in range(groups)])

    far, near = (3,), (2, 1, 0)
    combined, crossed = call(
        functools.partial(interact_far, late, far),
        (jax.ShapeDtypeStruct((classes, LEAD + DEPTH, spheres), jnp.bfloat16), shape(jnp.bfloat16)),
        len(late) * gather + len(far) * product,
        early,
        *(visiting[s] for s in late),
        table,
        weights,
        extra,
    )
    crossed = exchange(crossed, 1)
    ahead, beside, field = call(
        functools.partial(interact_near, near),
        (shape(jnp.float32), shape(jnp.bfloat16), shape(jnp.float32)),
        len(near) * product,
        weights,
        extra,
        combined,
    )
    ahead = exchange((ahead + crossed.astype(jnp.float32)).astype(jnp.bfloat16), 2)
    beside = exchange(beside, 1)
    field = field + beside.astype(jnp.float32) + ahead.astype(jnp.float32)
    return source.astype(jnp.float32) - mie_factor * field


def solution(mesh):
    return jax.shard_map(
        local,
        mesh=mesh,
        in_specs=(
            P("deg", "blk"),
            P(),
            P("deg", "blk"),
            P(None, None, "blk"),
            P(None, None, "blk"),
            P(None, None, "blk"),
        ),
        out_specs=P("deg", "blk"),
        check_vma=False,
    )
```

profile of v0, /device:TPU:69, one launch (start us, length us, event | category | flops | bytes accessed | tf_op | source)
XLA Modules:
  0.0 28.9 jit_solution(2697037855368655742)
XLA Ops:
  0.0 2.9 %collective-permute-start.2 = (bf16[168,256]{1,0:T(8,128)(2,1)}, bf16[168,256]{1,0:T(8,128)(2,1)S(1)}, u32[]{:S(2)}, u32[]{:S(2)}) collective-permute-start(bf16[168,256]{1,0:T(8,128)(2,1)} %refs_0_.1), channel_id=1, source_target_pairs={{0,12},{4,16},{8,20},{12,24},{16,28},{20,32},{24,36},{28,40},{32,4... | collective-permute-start | bytes 258056 | tf_op jit(solution)/shard_map/ppermute | solution.py:158
  2.9 2.5 %collective-permute-start.1 = (bf16[168,256]{1,0:T(8,128)(2,1)}, bf16[168,256]{1,0:T(8,128)(2,1)S(1)}, u32[]{:S(2)}, u32[]{:S(2)}) collective-permute-start(bf16[168,256]{1,0:T(8,128)(2,1)} %refs_0_.1), channel_id=1, source_target_pairs={{0,8},{4,12},{8,16},{12,20},{16,24},{20,28},{24,32},{28,36},{32,40... | collective-permute-start | bytes 258056 | tf_op jit(solution)/shard_map/ppermute | solution.py:158
  5.3 0.7 %collective-permute-start = (bf16[168,256]{1,0:T(8,128)(2,1)}, bf16[168,256]{1,0:T(8,128)(2,1)S(1)}, u32[]{:S(2)}, u32[]{:S(2)}) collective-permute-start(bf16[168,256]{1,0:T(8,128)(2,1)} %refs_0_.1), channel_id=1, source_target_pairs={{0,4},{4,8},{8,12},{12,16},{16,20},{20,24},{24,28},{28,32},{32,36}... | collective-permute-start | bytes 258056 | tf_op jit(solution)/shard_map/ppermute | solution.py:158
  6.1 4.4 %collective-permute-start.4 = (bf16[168,256]{1,0:T(8,128)(2,1)}, bf16[168,256]{1,0:T(8,128)(2,1)S(1)}, u32[]{:S(2)}, u32[]{:S(2)}) collective-permute-start(bf16[168,256]{1,0:T(8,128)(2,1)} %refs_0_.1), channel_id=1, source_target_pairs={{0,20},{4,24},{8,28},{12,32},{16,36},{20,40},{24,44},{28,48},{32,5... | collective-permute-start | bytes 258056 | tf_op jit(solution)/shard_map/ppermute | solution.py:158
  10.5 2.6 %collective-permute-start.3 = (bf16[168,256]{1,0:T(8,128)(2,1)}, bf16[168,256]{1,0:T(8,128)(2,1)S(1)}, u32[]{:S(2)}, u32[]{:S(2)}) collective-permute-start(bf16[168,256]{1,0:T(8,128)(2,1)} %refs_0_.1), channel_id=1, source_target_pairs={{0,16},{4,20},{8,24},{12,28},{16,32},{20,36},{24,40},{28,44},{32,4... | collective-permute-start | bytes 258056 | tf_op jit(solution)/shard_map/ppermute | solution.py:158
  13.1 0.8 %convert_add_fusion.codes = s32[6,4,256]{2,1,0:T(4,128)S(1)} fusion(bf16[6,4,256]{2,1,0:T(4,128)(2,1)} %param.11, s32[6,4,256]{2,1,0:T(4,128)} %param.9, s32[6,4,256]{2,1,0:T(4,128)} %param.10), kind=kLoop, calls=%fused_computation.2 | loop fusion | flops 43008 | bytes 86016 | tf_op jit(solution)/shard_map/add | solution.py:161
  13.9 0.0 copy-start
  13.9 3.2 %prepare.1 = (bf16[12,6,256,256]{3,2,1,0:T(8,128)(2,1)S(1)}, bf16[12,672,256]{2,1,0:T(8,128)(2,1)S(1)}, bf16[672,96]{1,0:T(8,128)(2,1)S(1)}) custom-call(s32[6,4,256]{2,1,0:T(4,128)S(1)} %convert_add_fusion.codes, bf16[12,672,672]{2,1,0:T(8,128)(2,1)} %operators.1), custom_call_target="tpu_custom_call" | custom-call | flops 1820786688 | bytes 10838016 | tf_op jit(solution)/shard_map/prepare/pallas_call | solution.py:162
  17.1 0.0 collective-permute-done.2.refs_3_
  17.1 0.0 collective-permute-done.1.refs_2_
  17.2 0.0 collective-permute-done.refs_1_
  17.2 0.0 copy-done
  17.2 1.3 %shard_map.64.refs_0_ = f32[12,168,256]{2,1,0:T(8,128)S(1)} custom-call(bf16[168,256]{1,0:T(8,128)(2,1)S(1)} %copy-done, bf16[168,256]{1,0:T(8,128)(2,1)S(1)} %collective-permute-done.refs_1_, bf16[168,256]{1,0:T(8,128)(2,1)S(1)} %collective-permute-done.1.refs_2_, bf16[168,256]{1,0:T(8,128)(2,1)S(1)} %collective-permute-done.2.refs_3_, ...), custom_call_target="tpu_custom_call" | custom-call | flops 1056964608 | bytes 86016 | tf_op jit(solution)/shard_map/pallas_call | solution.py:183
  18.5 0.0 collective-permute-done.4.refs_2_
  18.5 0.0 collective-permute-done.3.refs_1_
  18.5 1.7 %shard_map.65 = (bf16[12,264,256]{2,1,0:T(8,128)(2,1)S(1)}, bf16[168,256]{1,0:T(8,128)(2,1)S(1)}) custom-call(f32[12,168,256]{2,1,0:T(8,128)S(1)} %shard_map.64.refs_0_, bf16[168,256]{1,0:T(8,128)(2,1)S(1)} %collective-permute-done.3.refs_1_, bf16[168,256]{1,0:T(8,128)(2,1)S(1)} %collective-permute-done.4.refs_2_, ...), custom_call_target="tpu_custom_call" | custom-call | flops 701890560 | bytes 86016 | tf_op jit(solution)/shard_map/pallas_call | solution.py:183
  20.2 0.0 copy-start.1
  20.2 2.2 %collective-permute-start.6 = (bf16[168,256]{1,0:T(8,128)(2,1)S(1)}, bf16[168,256]{1,0:T(8,128)(2,1)S(1)}, u32[]{:S(2)}, u32[]{:S(2)}) collective-permute-start(bf16[168,256]{1,0:T(8,128)(2,1)S(1)} %get-tuple-element.20), channel_id=1, source_target_pairs={{0,1},{1,0},{2,3},{3,2},{4,5},{5,4},{6,7},{7,6},{8,9},{9,8},{10,11... | collective-permute-start | bytes 258056 | tf_op jit(solution)/shard_map/ppermute | solution.py:207
  22.4 1.1 %shard_map.66 = (f32[168,256]{1,0:T(8,128)S(1)}, bf16[168,256]{1,0:T(8,128)(2,1)S(1)}, f32[168,256]{1,0:T(8,128)S(1)}) custom-call(bf16[12,672,256]{2,1,0:T(8,128)(2,1)S(1)} %get-tuple-element.13.refs_4_.weights, bf16[672,96]{1,0:T(8,128)(2,1)S(1)} %get-tuple-element.14.refs_5_.extra, bf16[12,264,256]{2,1,0:T(8,128)(2,1)S(1)} %get-tuple-element.16.combined), custom_call_target="tpu_custom_call" | custom-call | flops 520224768 | bytes 86016 | tf_op jit(solution)/shard_map/pallas_call | solution.py:183
  23.5 0.1 collective-permute-start.5
  23.6 0.0 collective-permute-done.6
  23.6 2.0 %collective-permute-start.7 = (bf16[168,256]{1,0:T(8,128)(2,1)S(1)}, bf16[168,256]{1,0:T(8,128)(2,1)S(1)}, u32[]{:S(2)}, u32[]{:S(2)}) collective-permute-start(bf16[168,256]{1,0:T(8,128)(2,1)S(1)} %add_convert_fusion), channel_id=1, source_target_pairs={{0,2},{1,3},{2,0},{3,1},{4,6},{5,7},{6,4},{7,5},{8,10},{9,11},{10,... | collective-permute-start | bytes 258056 | tf_op jit(solution)/shard_map/ppermute | solution.py:207
  25.6 0.0 collective-permute-done.5
  25.6 2.6 %collective-permute-done.7 = bf16[168,256]{1,0:T(8,128)(2,1)S(1)} collective-permute-done((bf16[168,256]{1,0:T(8,128)(2,1)S(1)}, bf16[168,256]{1,0:T(8,128)(2,1)S(1)}, u32[]{:S(2)}, u32[]{:S(2)}) %collective-permute-start.7) | collective-permute-done | bytes 86048 | tf_op jit(solution)/shard_map/ppermute | solution.py:207
  28.2 0.0 copy-done.1
  28.2 0.7 %multiply_subtract_fusion = f32[168,256]{1,0:T(8,128)} fusion(f32[168,256]{1,0:T(8,128)S(1)} %copy-done.1, bf16[168,256]{1,0:T(8,128)(2,1)S(1)} %collective-permute-done.7, f32[168,256]{1,0:T(8,128)S(1)} %get-tuple-element.17, bf16[168,256]{1,0:T(8,128)(2,1)S(1)} %collective-permute-done.5, bf16[168,256]{1,0:T(8,128)(2,1)S(1)} %copy-done), kind=kLoop, calls=%fused_computation | loop fusion | flops 301056 | bytes 774144 | tf_op jit(solution)/shard_map/sub | solution.py:232
  (1 shorter events, 0.0 us)
Async XLA Ops:
  0.0 17.1 %collective-permute-start.2 = (bf16[168,256]{1,0:T(8,128)(2,1)}, bf16[168,256]{1,0:T(8,128)(2,1)S(1)}, u32[]{:S(2)}, u32[]{:S(2)}) collective-permute-start(bf16[168,256]{1,0:T(8,128)(2,1)} %refs_0_.1), channel_id=1, source_target_pairs={{0,12},{4,16},{8,20},{12,24},{16,28},{20,32},{24,36},{28,40},{32,4... | collective-permute-start | bytes 258056 | tf_op jit(solution)/shard_map/ppermute | solution.py:158
  2.9 14.3 %collective-permute-start.1 = (bf16[168,256]{1,0:T(8,128)(2,1)}, bf16[168,256]{1,0:T(8,128)(2,1)S(1)}, u32[]{:S(2)}, u32[]{:S(2)}) collective-permute-start(bf16[168,256]{1,0:T(8,128)(2,1)} %refs_0_.1), channel_id=1, source_target_pairs={{0,8},{4,12},{8,16},{12,20},{16,24},{20,28},{24,32},{28,36},{32,40... | collective-permute-start | bytes 258056 | tf_op jit(solution)/shard_map/ppermute | solution.py:158
  5.3 11.8 %collective-permute-start = (bf16[168,256]{1,0:T(8,128)(2,1)}, bf16[168,256]{1,0:T(8,128)(2,1)S(1)}, u32[]{:S(2)}, u32[]{:S(2)}) collective-permute-start(bf16[168,256]{1,0:T(8,128)(2,1)} %refs_0_.1), channel_id=1, source_target_pairs={{0,4},{4,8},{8,12},{12,16},{16,20},{20,24},{24,28},{28,32},{32,36}... | collective-permute-start | bytes 258056 | tf_op jit(solution)/shard_map/ppermute | solution.py:158
  6.1 12.4 %collective-permute-start.4 = (bf16[168,256]{1,0:T(8,128)(2,1)}, bf16[168,256]{1,0:T(8,128)(2,1)S(1)}, u32[]{:S(2)}, u32[]{:S(2)}) collective-permute-start(bf16[168,256]{1,0:T(8,128)(2,1)} %refs_0_.1), channel_id=1, source_target_pairs={{0,20},{4,24},{8,28},{12,32},{16,36},{20,40},{24,44},{28,48},{32,5... | collective-permute-start | bytes 258056 | tf_op jit(solution)/shard_map/ppermute | solution.py:158
  10.5 8.0 %collective-permute-start.3 = (bf16[168,256]{1,0:T(8,128)(2,1)}, bf16[168,256]{1,0:T(8,128)(2,1)S(1)}, u32[]{:S(2)}, u32[]{:S(2)}) collective-permute-start(bf16[168,256]{1,0:T(8,128)(2,1)} %refs_0_.1), channel_id=1, source_target_pairs={{0,16},{4,20},{8,24},{12,28},{16,32},{20,36},{24,40},{28,44},{32,4... | collective-permute-start | bytes 258056 | tf_op jit(solution)/shard_map/ppermute | solution.py:158
  13.9 3.2 %copy-start = (bf16[168,256]{1,0:T(8,128)(2,1)S(1)}, bf16[168,256]{1,0:T(8,128)(2,1)}, u32[]{:S(2)}) copy-start(bf16[168,256]{1,0:T(8,128)(2,1)} %refs_0_.1) | copy-start | bytes 258052
  20.2 7.9 %copy-start.1 = (f32[168,256]{1,0:T(8,128)S(1)}, f32[168,256]{1,0:T(8,128)}, u32[]{:S(2)}) copy-start(f32[168,256]{1,0:T(8,128)} %param.8) | copy-start | bytes 516100
  20.2 3.3 %collective-permute-start.6 = (bf16[168,256]{1,0:T(8,128)(2,1)S(1)}, bf16[168,256]{1,0:T(8,128)(2,1)S(1)}, u32[]{:S(2)}, u32[]{:S(2)}) collective-permute-start(bf16[168,256]{1,0:T(8,128)(2,1)S(1)} %get-tuple-element.20), channel_id=1, source_target_pairs={{0,1},{1,0},{2,3},{3,2},{4,5},{5,4},{6,7},{7,6},{8,9},{9,8},{10,11... | collective-permute-start | bytes 258056 | tf_op jit(solution)/shard_map/ppermute | solution.py:207
  23.5 2.1 %collective-permute-start.5 = (bf16[168,256]{1,0:T(8,128)(2,1)S(1)}, bf16[168,256]{1,0:T(8,128)(2,1)S(1)}, u32[]{:S(2)}, u32[]{:S(2)}) collective-permute-start(bf16[168,256]{1,0:T(8,128)(2,1)S(1)} %get-tuple-element.18), channel_id=1, source_target_pairs={{0,1},{1,0},{2,3},{3,2},{4,5},{5,4},{6,7},{7,6},{8,9},{9,8},{10,11... | collective-permute-start | bytes 258056 | tf_op jit(solution)/shard_map/ppermute | solution.py:207
  23.6 4.6 %collective-permute-start.7 = (bf16[168,256]{1,0:T(8,128)(2,1)S(1)}, bf16[168,256]{1,0:T(8,128)(2,1)S(1)}, u32[]{:S(2)}, u32[]{:S(2)}) collective-permute-start(bf16[168,256]{1,0:T(8,128)(2,1)S(1)} %add_convert_fusion), channel_id=1, source_target_pairs={{0,2},{1,3},{2,0},{3,1},{4,6},{5,7},{6,4},{7,5},{8,10},{9,11},{10,... | collective-permute-start | bytes 258056 | tf_op jit(solution)/shard_map/ppermute | solution.py:207
where the time goes:
time: 29.4 us; the launch traced here: 28.9 us
  starting transfers between devices  17.4 us (59%)
  Pallas kernels  7.26 us (25%)
  waiting for transfers between devices  2.6 us (9%)
  other arithmetic  1.54 us (5%)
    ppermute x5, starting transfers between devices, local(): lax.ppermute(source, 'blk', [(b, (b + s) % blocks) for b in range(blocks)])  13.1 us
    ppermute x3, starting transfers between devices, exchange(): return lax.ppermute(x, 'deg', [(i, i ^ distance) for i in range(groups)])  4.25 us
    pallas_call x3, Pallas kernels, call(): pl.pallas_call(kernel, out_shape=out_shape, in_specs=[VMEM] * len(operand...  4.07 us
    pallas_call x1, Pallas kernels, local(): pl.pallas_call(prepare, out_shape=(jax.ShapeDtypeStruct((classes, visits,...  3.2 us
    ppermute x3, waiting for transfers between devices, exchange(): return lax.ppermute(x, 'deg', [(i, i ^ distance) for i in range(groups)])  2.58 us
    add x1, other arithmetic, local(): (pair_class * 2 ** SPHERE_BITS + pair_source) * 2 ** SCALE_BITS + units  0.79 us
    sub x1, other arithmetic, local(): return source.astype(jnp.float32) - mie_factor * field  0.73 us
  transfers between devices with their start and end apart: 8, of which 1 were waited for; matrix products, arithmetic and copies ran while one was open for 3% of the time, Pallas kernels for 19%

commit v1 on v0

--- a/solution.py
+++ b/solution.py
@@ -9,9 +9,9 @@
 
 
 LANES = 128
-STRIP = 64
-ORDER = (0, 1, 2, 3, 4, 5)
-EARLY = 4
+STRIP = 32
+ORDER = (0, 1, 3, 2, 4, 5)
+EARLY = 3
 SPHERE_BITS = 8
 SCALE_BITS = 10
 SCALE_UNIT = 512

time: 29.4 us -> 30.1 us (1.024)
  starting transfers between devices: 17.4 us -> 18 us
    ppermute x5, starting transfers between devices: 13.1 us -> 13.7 us  [local(): lax.ppermute(source, 'blk', [(b, (b + s) % blocks) for b in range(blocks)])]
  transfers between devices with their start and end apart: 8 -> 8, of which waited for: 1 -> 1; matrix products, arithmetic and copies ran while one was open for 3% -> 3% of each run, Pallas kernels for 19% -> 18%
where the time goes in v1:
time: 30.1 us; the launch traced here: 29.5 us
  starting transfers between devices  18 us (60%)
  Pallas kernels  7.29 us (24%)
  waiting for transfers between devices  2.6 us (9%)
  other arithmetic  1.54 us (5%)
    ppermute x5, starting transfers between devices, local(): lax.ppermute(source, 'blk', [(b, (b + s) % blocks) for b in range(blocks)])  13.7 us
    ppermute x3, starting transfers between devices, exchange(): return lax.ppermute(x, 'deg', [(i, i ^ distance) for i in range(groups)])  4.26 us
    pallas_call x3, Pallas kernels, call(): pl.pallas_call(kernel, out_shape=out_shape, in_specs=[VMEM] * len(operand...  4.07 us
    pallas_call x1, Pallas kernels, local(): pl.pallas_call(prepare, out_shape=(jax.ShapeDtypeStruct((classes, visits,...  3.21 us
    ppermute x3, waiting for transfers between devices, exchange(): return lax.ppermute(x, 'deg', [(i, i ^ distance) for i in range(groups)])  2.59 us
    add x1, other arithmetic, local(): (pair_class * 2 ** SPHERE_BITS + pair_source) * 2 ** SCALE_BITS + units  0.79 us
    sub x1, other arithmetic, local(): return source.astype(jnp.float32) - mie_factor * field  0.73 us
  transfers between devices with their start and end apart: 8, of which 1 were waited for; matrix products, arithmetic and copies ran while one was open for 3% of the time, Pallas kernels for 18%

profile of v1, /device:TPU:69, one launch (start us, length us, event | category | flops | bytes accessed | tf_op | source)
XLA Modules:
  0.0 29.5 jit_solution(7001464561571597565)
XLA Ops:
  0.0 2.9 %collective-permute-start.2 = (bf16[168,256]{1,0:T(8,128)(2,1)}, bf16[168,256]{1,0:T(8,128)(2,1)S(1)}, u32[]{:S(2)}, u32[]{:S(2)}) collective-permute-start(bf16[168,256]{1,0:T(8,128)(2,1)} %refs_0_.1), channel_id=1, source_target_pairs={{0,8},{4,12},{8,16},{12,20},{16,24},{20,28},{24,32},{28,36},{32,40... | collective-permute-start | bytes 258056 | tf_op jit(solution)/shard_map/ppermute | solution.py:158
  2.9 1.9 %collective-permute-start.1 = (bf16[168,256]{1,0:T(8,128)(2,1)}, bf16[168,256]{1,0:T(8,128)(2,1)S(1)}, u32[]{:S(2)}, u32[]{:S(2)}) collective-permute-start(bf16[168,256]{1,0:T(8,128)(2,1)} %refs_0_.1), channel_id=1, source_target_pairs={{0,12},{4,16},{8,20},{12,24},{16,28},{20,32},{24,36},{28,40},{32,4... | collective-permute-start | bytes 258056 | tf_op jit(solution)/shard_map/ppermute | solution.py:158
  4.7 0.7 %collective-permute-start = (bf16[168,256]{1,0:T(8,128)(2,1)}, bf16[168,256]{1,0:T(8,128)(2,1)S(1)}, u32[]{:S(2)}, u32[]{:S(2)}) collective-permute-start(bf16[168,256]{1,0:T(8,128)(2,1)} %refs_0_.1), channel_id=1, source_target_pairs={{0,4},{4,8},{8,12},{12,16},{16,20},{20,24},{24,28},{28,32},{32,36}... | collective-permute-start | bytes 258056 | tf_op jit(solution)/shard_map/ppermute | solution.py:158
  5.5 5.7 %collective-permute-start.4 = (bf16[168,256]{1,0:T(8,128)(2,1)}, bf16[168,256]{1,0:T(8,128)(2,1)S(1)}, u32[]{:S(2)}, u32[]{:S(2)}) collective-permute-start(bf16[168,256]{1,0:T(8,128)(2,1)} %refs_0_.1), channel_id=1, source_target_pairs={{0,20},{4,24},{8,28},{12,32},{16,36},{20,40},{24,44},{28,48},{32,5... | collective-permute-start | bytes 258056 | tf_op jit(solution)/shard_map/ppermute | solution.py:158
  11.1 2.6 %collective-permute-start.3 = (bf16[168,256]{1,0:T(8,128)(2,1)}, bf16[168,256]{1,0:T(8,128)(2,1)S(1)}, u32[]{:S(2)}, u32[]{:S(2)}) collective-permute-start(bf16[168,256]{1,0:T(8,128)(2,1)} %refs_0_.1), channel_id=1, source_target_pairs={{0,16},{4,20},{8,24},{12,28},{16,32},{20,36},{24,40},{28,44},{32,4... | collective-permute-start | bytes 258056 | tf_op jit(solution)/shard_map/ppermute | solution.py:158
  13.7 0.8 %convert_add_fusion.codes = s32[6,4,256]{2,1,0:T(4,128)S(1)} fusion(bf16[6,4,256]{2,1,0:T(4,128)(2,1)} %param.11, s32[6,4,256]{2,1,0:T(4,128)} %param.9, s32[6,4,256]{2,1,0:T(4,128)} %param.10), kind=kLoop, calls=%fused_computation.2 | loop fusion | flops 43008 | bytes 86016 | tf_op jit(solution)/shard_map/add | solution.py:161
  14.5 0.0 copy-start
  14.5 3.2 %prepare.1 = (bf16[12,6,256,256]{3,2,1,0:T(8,128)(2,1)S(1)}, bf16[12,672,256]{2,1,0:T(8,128)(2,1)S(1)}, bf16[672,96]{1,0:T(8,128)(2,1)S(1)}) custom-call(s32[6,4,256]{2,1,0:T(4,128)S(1)} %convert_add_fusion.codes, bf16[12,672,672]{2,1,0:T(8,128)(2,1)} %operators.1), custom_call_target="tpu_custom_call" | custom-call | flops 1820786688 | bytes 10838016 | tf_op jit(solution)/shard_map/prepare/pallas_call | solution.py:162
  17.8 0.0 collective-permute-done.1.refs_2_
  17.8 0.0 collective-permute-done.refs_1_
  17.8 0.0 copy-done
  17.8 1.0 %shard_map.64.refs_0_ = f32[12,168,256]{2,1,0:T(8,128)S(1)} custom-call(bf16[168,256]{1,0:T(8,128)(2,1)S(1)} %copy-done, bf16[168,256]{1,0:T(8,128)(2,1)S(1)} %collective-permute-done.refs_1_, bf16[168,256]{1,0:T(8,128)(2,1)S(1)} %collective-permute-done.1.refs_2_, bf16[12,6,256,256]{3,2,1,0:T(8,128)(2,1)S(1)} %get-tuple-element.15.refs_3_.refs_4_), custom_call_target="tpu_custom_call" | custom-call | flops 792723456 | bytes 86016 | tf_op jit(solution)/shard_map/pallas_call | solution.py:183
  18.8 0.0 collective-permute-done.2.refs_1_
  18.8 0.0 collective-permute-done.4.refs_3_
  18.8 0.0 collective-permute-done.3.refs_2_
  18.9 2.0 %shard_map.65 = (bf16[12,264,256]{2,1,0:T(8,128)(2,1)S(1)}, bf16[168,256]{1,0:T(8,128)(2,1)S(1)}) custom-call(f32[12,168,256]{2,1,0:T(8,128)S(1)} %shard_map.64.refs_0_, bf16[168,256]{1,0:T(8,128)(2,1)S(1)} %collective-permute-done.2.refs_1_, bf16[168,256]{1,0:T(8,128)(2,1)S(1)} %collective-permute-done.3.refs_2_, ...), custom_call_target="tpu_custom_call" | custom-call | flops 966131712 | bytes 86016 | tf_op jit(solution)/shard_map/pallas_call | solution.py:183
  20.9 0.0 copy-start.1
  20.9 2.2 %collective-permute-start.6 = (bf16[168,256]{1,0:T(8,128)(2,1)S(1)}, bf16[168,256]{1,0:T(8,128)(2,1)S(1)}, u32[]{:S(2)}, u32[]{:S(2)}) collective-permute-start(bf16[168,256]{1,0:T(8,128)(2,1)S(1)} %get-tuple-element.20), channel_id=1, source_target_pairs={{0,1},{1,0},{2,3},{3,2},{4,5},{5,4},{6,7},{7,6},{8,9},{9,8},{10,11... | collective-permute-start | bytes 258056 | tf_op jit(solution)/shard_map/ppermute | solution.py:207
  23.0 1.1 %shard_map.66 = (f32[168,256]{1,0:T(8,128)S(1)}, bf16[168,256]{1,0:T(8,128)(2,1)S(1)}, f32[168,256]{1,0:T(8,128)S(1)}) custom-call(bf16[12,672,256]{2,1,0:T(8,128)(2,1)S(1)} %get-tuple-element.13.refs_5_.weights, bf16[672,96]{1,0:T(8,128)(2,1)S(1)} %get-tuple-element.14.refs_6_.extra, bf16[12,264,256]{2,1,0:T(8,128)(2,1)S(1)} %get-tuple-element.16.combined), custom_call_target="tpu_custom_call" | custom-call | flops 520224768 | bytes 86016 | tf_op jit(solution)/shard_map/pallas_call | solution.py:183
  24.1 0.1 collective-permute-start.5
  24.2 0.0 collective-permute-done.6
  24.2 2.0 %collective-permute-start.7 = (bf16[168,256]{1,0:T(8,128)(2,1)S(1)}, bf16[168,256]{1,0:T(8,128)(2,1)S(1)}, u32[]{:S(2)}, u32[]{:S(2)}) collective-permute-start(bf16[168,256]{1,0:T(8,128)(2,1)S(1)} %add_convert_fusion), channel_id=1, source_target_pairs={{0,2},{1,3},{2,0},{3,1},{4,6},{5,7},{6,4},{7,5},{8,10},{9,11},{10,... | collective-permute-start | bytes 258056 | tf_op jit(solution)/shard_map/ppermute | solution.py:207
  26.2 0.0 collective-permute-done.5
  26.2 2.6 %collective-permute-done.7 = bf16[168,256]{1,0:T(8,128)(2,1)S(1)} collective-permute-done((bf16[168,256]{1,0:T(8,128)(2,1)S(1)}, bf16[168,256]{1,0:T(8,128)(2,1)S(1)}, u32[]{:S(2)}, u32[]{:S(2)}) %collective-permute-start.7) | collective-permute-done | bytes 86048 | tf_op jit(solution)/shard_map/ppermute | solution.py:207
  28.8 0.0 copy-done.1
  28.8 0.7 %multiply_subtract_fusion = f32[168,256]{1,0:T(8,128)} fusion(f32[168,256]{1,0:T(8,128)S(1)} %copy-done.1, bf16[168,256]{1,0:T(8,128)(2,1)S(1)} %collective-permute-done.7, f32[168,256]{1,0:T(8,128)S(1)} %get-tuple-element.17, bf16[168,256]{1,0:T(8,128)(2,1)S(1)} %collective-permute-done.5, bf16[168,256]{1,0:T(8,128)(2,1)S(1)} %copy-done), kind=kLoop, calls=%fused_computation | loop fusion | flops 301056 | bytes 774144 | tf_op jit(solution)/shard_map/sub | solution.py:232
  (1 shorter events, 0.0 us)
Async XLA Ops:
  0.0 18.8 %collective-permute-start.2 = (bf16[168,256]{1,0:T(8,128)(2,1)}, bf16[168,256]{1,0:T(8,128)(2,1)S(1)}, u32[]{:S(2)}, u32[]{:S(2)}) collective-permute-start(bf16[168,256]{1,0:T(8,128)(2,1)} %refs_0_.1), channel_id=1, source_target_pairs={{0,8},{4,12},{8,16},{12,20},{16,24},{20,28},{24,32},{28,36},{32,40... | collective-permute-start | bytes 258056 | tf_op jit(solution)/shard_map/ppermute | solution.py:158
  2.9 14.9 %collective-permute-start.1 = (bf16[168,256]{1,0:T(8,128)(2,1)}, bf16[168,256]{1,0:T(8,128)(2,1)S(1)}, u32[]{:S(2)}, u32[]{:S(2)}) collective-permute-start(bf16[168,256]{1,0:T(8,128)(2,1)} %refs_0_.1), channel_id=1, source_target_pairs={{0,12},{4,16},{8,20},{12,24},{16,28},{20,32},{24,36},{28,40},{32,4... | collective-permute-start | bytes 258056 | tf_op jit(solution)/shard_map/ppermute | solution.py:158
  4.7 13.0 %collective-permute-start = (bf16[168,256]{1,0:T(8,128)(2,1)}, bf16[168,256]{1,0:T(8,128)(2,1)S(1)}, u32[]{:S(2)}, u32[]{:S(2)}) collective-permute-start(bf16[168,256]{1,0:T(8,128)(2,1)} %refs_0_.1), channel_id=1, source_target_pairs={{0,4},{4,8},{8,12},{12,16},{16,20},{20,24},{24,28},{28,32},{32,36}... | collective-permute-start | bytes 258056 | tf_op jit(solution)/shard_map/ppermute | solution.py:158
  5.5 13.4 %collective-permute-start.4 = (bf16[168,256]{1,0:T(8,128)(2,1)}, bf16[168,256]{1,0:T(8,128)(2,1)S(1)}, u32[]{:S(2)}, u32[]{:S(2)}) collective-permute-start(bf16[168,256]{1,0:T(8,128)(2,1)} %refs_0_.1), channel_id=1, source_target_pairs={{0,20},{4,24},{8,28},{12,32},{16,36},{20,40},{24,44},{28,48},{32,5... | collective-permute-start | bytes 258056 | tf_op jit(solution)/shard_map/ppermute | solution.py:158
  11.1 7.7 %collective-permute-start.3 = (bf16[168,256]{1,0:T(8,128)(2,1)}, bf16[168,256]{1,0:T(8,128)(2,1)S(1)}, u32[]{:S(2)}, u32[]{:S(2)}) collective-permute-start(bf16[168,256]{1,0:T(8,128)(2,1)} %refs_0_.1), channel_id=1, source_target_pairs={{0,16},{4,20},{8,24},{12,28},{16,32},{20,36},{24,40},{28,44},{32,4... | collective-permute-start | bytes 258056 | tf_op jit(solution)/shard_map/ppermute | solution.py:158
  14.5 3.3 %copy-start = (bf16[168,256]{1,0:T(8,128)(2,1)S(1)}, bf16[168,256]{1,0:T(8,128)(2,1)}, u32[]{:S(2)}) copy-start(bf16[168,256]{1,0:T(8,128)(2,1)} %refs_0_.1) | copy-start | bytes 258052
  20.9 8.0 %copy-start.1 = (f32[168,256]{1,0:T(8,128)S(1)}, f32[168,256]{1,0:T(8,128)}, u32[]{:S(2)}) copy-start(f32[168,256]{1,0:T(8,128)} %param.8) | copy-start | bytes 516100
  20.9 3.3 %collective-permute-start.6 = (bf16[168,256]{1,0:T(8,128)(2,1)S(1)}, bf16[168,256]{1,0:T(8,128)(2,1)S(1)}, u32[]{:S(2)}, u32[]{:S(2)}) collective-permute-start(bf16[168,256]{1,0:T(8,128)(2,1)S(1)} %get-tuple-element.20), channel_id=1, source_target_pairs={{0,1},{1,0},{2,3},{3,2},{4,5},{5,4},{6,7},{7,6},{8,9},{9,8},{10,11... | collective-permute-start | bytes 258056 | tf_op jit(solution)/shard_map/ppermute | solution.py:207
  24.1 2.1 %collective-permute-start.5 = (bf16[168,256]{1,0:T(8,128)(2,1)S(1)}, bf16[168,256]{1,0:T(8,128)(2,1)S(1)}, u32[]{:S(2)}, u32[]{:S(2)}) collective-permute-start(bf16[168,256]{1,0:T(8,128)(2,1)S(1)} %get-tuple-element.18), channel_id=1, source_target_pairs={{0,1},{1,0},{2,3},{3,2},{4,5},{5,4},{6,7},{7,6},{8,9},{9,8},{10,11... | collective-permute-start | bytes 258056 | tf_op jit(solution)/shard_map/ppermute | solution.py:207
  24.2 4.6 %collective-permute-start.7 = (bf16[168,256]{1,0:T(8,128)(2,1)S(1)}, bf16[168,256]{1,0:T(8,128)(2,1)S(1)}, u32[]{:S(2)}, u32[]{:S(2)}) collective-permute-start(bf16[168,256]{1,0:T(8,128)(2,1)S(1)} %add_convert_fusion), channel_id=1, source_target_pairs={{0,2},{1,3},{2,0},{3,1},{4,6},{5,7},{6,4},{7,5},{8,10},{9,11},{10,... | collective-permute-start | bytes 258056 | tf_op jit(solution)/shard_map/ppermute | solution.py:207
